TPU v7x, 32 devices: a whole 2x2x4 slice. The times are simulated.
32 devices in a mesh: term: 4 (over y, x), sector: 8 (over z, core).
Axes of the slice: x: 2, y: 2, z: 4, core: 2. Of those that a mesh axis runs over, the one named last changes fastest.
Arguments:
- wavefunction: float32 [8, 512, 512], P('sector'), may hold values from -120 to 120
- precond: float32 [8, 512, 512], P('sector', 'term'), may hold values from 0.05 to 4
- left_ops: float32 [8, 16, 512, 512], P('sector', 'term'), may hold values from -0.5 to 4.5
- right_ops: float32 [8, 16, 512, 512], P('sector', 'term'), may hold values from -1 to 2
- out_sector: int32 [8, 16], P('sector', 'term'), may hold values from 0 to 7, as said below
- live_counts: int32 [8, 4], P('sector', 'term'), may hold values from 1 to 4, as said below
Outputs:
- first_image: float32 [8, 512, 512], P('sector', 'term')
- correction: float32 [8, 512, 512], P('sector', 'term')
- second_image: float32 [8, 512, 512], P('sector', 'term')
Inputs may be any that keep to these rules, and one draw needn't show every extreme that they name: Each term moves the charge by at most one sector: out_sector[s, j] differs from s by at most 1. `live_counts`: in every sector some device has all 4 slots live.
All inputs are finite; a program needn't handle non-finite values.
Results may differ from a plain program's by a relative error of at most 0.0003.
Values sent between devices are 32-bit elements; how exact they have to be, the bound alone decides.
A program may use at most 64 MiB of HBM per device.

v0:
```python
import jax
import jax.numpy as jnp
from jax import lax
from jax.sharding import PartitionSpec as P


def from_behind(block, axis, distance):
    devices = range(lax.axis_size(axis))
    route = [(i - distance, i) for i in devices if i - distance in devices]
    return lax.ppermute(block, axis, route)


def matmul(first_op, second_op):
    return jnp.dot(
        first_op, second_op, precision=lax.Precision.HIGHEST, preferred_element_type=jnp.float32
    )


def term_rows(vector, left_stack, right_stack, offsets, kept, row_count):
    width = vector.shape[1]
    totals = jnp.zeros((row_count, 3, width), jnp.float32)

    def add_slot(slot_id, running):
        left_rows = left_stack[slot_id]
        product = matmul(matmul(left_rows, vector), right_stack[slot_id])
        return running.at[:, offsets[slot_id]].add(product)

    totals = lax.fori_loop(jnp.zeros((), jnp.int32), kept, add_slot, totals)
    return totals.reshape(row_count, 3 * width)


def per_device(wavefunction, precond, left_ops, right_ops, out_sector, live_counts):
    term_count = lax.axis_size("term")
    width = wavefunction.shape[1]
    slab_rows = width // term_count
    first_own = lax.axis_index("term") * slab_rows
    sector_id = lax.axis_index("sector")
    center = wavefunction[0]
    left_stack = left_ops[0]
    right_stack = right_ops[0]
    offsets = out_sector[0] - sector_id + 1
    count_here = live_counts[0, 0]

    def apply_hamiltonian(vector):
        whole = term_rows(vector, left_stack, right_stack, offsets, count_here, width).reshape(
            width, 3, width
        )
        upward = from_behind(whole[:, 2], "sector", 1)
        downward = from_behind(whole[:, 0], "sector", -1)
        return lax.psum_scatter(
            whole[:, 1] + upward + downward, "term", scatter_dimension=0, tiled=True
        )

    first_image = apply_hamiltonian(center)
    own_rows = lax.dynamic_slice_in_dim(center, first_own, slab_rows, 0)
    scaling = precond[0]
    cross, norm_sq = lax.psum(
        (jnp.sum(own_rows * first_image), jnp.sum(own_rows * own_rows)), ("term", "sector")
    )
    rayleigh = cross / norm_sq
    raw = scaling * (first_image - rayleigh * own_rows)
    correlation_sum = lax.psum(jnp.sum(own_rows * raw), ("term", "sector"))
    correction = raw - correlation_sum / norm_sq * own_rows
    full_correction = lax.all_gather(correction, "term", axis=0, tiled=True)
    second_image = apply_hamiltonian(full_correction)
    return (first_image[None], correction[None], second_image[None])


def solution(mesh):
    placed = (
        P("sector", None, None),
        P("sector", "term", None),
        P("sector", "term", None, None),
        P("sector", "term", None, None),
        P("sector", "term"),
        P("sector", "term"),
    )
    return jax.shard_map(
        per_device,
        mesh=mesh,
        in_specs=placed,
        out_specs=(P("sector", "term", None), P("sector", "term", None), P("sector", "term", None)),
        check_vma=False,
    )
```

profile of v0, /device:TPU:0, one launch (start us, length us, event | category | flops | bytes accessed | tf_op | source)
XLA Modules:
  0.0 316.2 jit_solution(16993770695380085301)
XLA Ops:
  7.2 0.0 copy-start.1
  7.2 0.0 reduce-scatter.3.cloned.1.call-start
  7.2 0.7 add_bitcast_fusion
  7.9 0.4 broadcast.48.clone
  8.3 0.0 copy-done.1
  8.3 11.7 %while.22 = (s32[]{:T(128)}, f32[512,3,512]{2,0,1:T(8,128)S(1)}, s32[]{:T(128)}, s32[4]{0:T(128)S(1)}, f32[4,512,512]{2,1,0:T(8,128)}, /*index=5*/f32[512,512]{1...) while((s32[]{:T(128)}, f32[512,3,512]{2,0,1:T(8,128)S(1)}, ...), condition=%wide.region_2.0_spmd, body=%wide.region_0.0_spmd.sunk | while | flops 3221749760 | bytes 7341298 | solution.py:28
  9.0 0.6 dynamic_slice.53
  11.5 0.7 and_reduce_fusion.4
  12.2 3.4 %fusion.44 = f32[512,512]{1,0:T(8,128)S(1)} fusion(f32[512,512]{1,0:T(8,128)} %get-tuple-element.260, f32[4,512,512]{2,1,0:T(8,128)} %get-tuple-element.259, s32[]{:T(128)S(6)} %select_n.28), kind=kOutput, calls=%fused_computation.4.clone.1 | convolution fusion | flops 1610612736 | bytes 3145732 | tf_op jit(solution)/shard_map/while/body/dot_general | solution.py:14
  15.6 3.8 %fusion.45 = f32[512,3,512]{2,0,1:T(8,128)S(1)} fusion(f32[512,3,512]{2,0,1:T(8,128)S(1)} %get-tuple-element.243, s32[]{:T(128)} %select_n.29, f32[512,512]{1,0:T(8,128)S(1)} %fusion.44, f32[4,512,512]{2,1,0:T(8,128)} %get-tuple-element.261, s32[]{:T(128)S(6)} %select_n.28, pred[]{:T(512)} %and_reduce_fusion.4), kind=kOutput, calls=%fused_computation.2.clone.1 | convolution fusion | flops 1611137024 | bytes 4195332 | tf_op jit(solution)/shard_map/while/body/dot_general | solution.py:14
  20.0 0.2 slice_bitcast_fusion.3
  20.2 0.0 copy-start
  20.2 2.6 collective-permute-start
  22.8 1.3 collective-permute-start.1
  24.1 0.9 collective-permute-done
  25.0 4.5 %collective-permute-done.1 = f32[512,512]{1,0:T(8,128)S(1)} collective-permute-done((f32[512,512]{1,0:T(8,128)S(1)}, f32[512,512]{1,0:T(8,128)S(1)}, u32[]{:S(2)}, u32[]{:S(2)}) %collective-permute-start.1) | collective-permute-done | bytes 1048608 | tf_op jit(solution)/shard_map/ppermute | solution.py:10
  29.5 1.4 fusion.17
  30.9 0.0 reduce-scatter.3.cloned.1.call-update
  30.9 0.0 all-gather.2.cloned.1.call-start
  30.9 72.2 %reduce-scatter.3.cloned.1.call-done = f32[128,512]{1,0:T(8,128)} async-done(((f32[512,512]{1,0:T(8,128)}), f32[128,512]{1,0:T(8,128)}) %reduce-scatter.3.cloned.1.call-update) | async-done | bytes 262160 | tf_op jit(solution)/shard_map/reduce_scatter | solution.py:50
  103.2 1.7 fusion.19
  104.9 39.5 %all-reduce = (f32[]{:T(128)}, f32[]{:T(128)}) all-reduce(f32[]{:T(128)} %get-tuple-element.106, f32[]{:T(128)} %get-tuple-element.105), channel_id=1, replica_groups=mesh['term'=4,'sector'=8] {'term','sector'}, use_global_device_ids=true, to_apply=%region_5.0 | all-reduce | flops 2 | bytes 16 | tf_op jit(solution)/shard_map/psum | solution.py:57
  145.7 0.0 copy-done
  145.7 1.7 fusion.22
  147.5 41.3 %psum.23 = f32[]{:T(128)} all-reduce(f32[]{:T(128)} %fusion.22), channel_id=1, replica_groups=mesh['term'=4,'sector'=8] {'term','sector'}, use_global_device_ids=true, to_apply=%region_9.0 | all-reduce | flops 1 | bytes 8 | tf_op jit(solution)/shard_map/psum | solution.py:62
  190.1 1.8 fusion.23
  191.9 0.0 all-gather.2.cloned.1.call-update
  192.0 0.0 reduce-scatter.5.cloned.1.call-start
  192.0 26.5 %all-gather.2.cloned.1.call-done = f32[512,512]{1,0:T(8,128)} async-done(((f32[128,512]{1,0:T(8,128)}), f32[512,512]{1,0:T(8,128)}) %all-gather.2.cloned.1.call-update) | async-done | bytes 1048592 | tf_op jit(solution)/shard_map/all_gather | solution.py:64
  218.6 0.4 broadcast.48
  218.9 11.4 %while.23 = (s32[]{:T(128)}, f32[512,3,512]{2,0,1:T(8,128)S(1)}, s32[]{:T(128)}, s32[4]{0:T(128)S(1)}, f32[4,512,512]{2,1,0:T(8,128)}, /*index=5*/f32[512,512]{1...) while((s32[]{:T(128)}, f32[512,3,512]{2,0,1:T(8,128)S(1)}, ...), condition=%wide.region_12.0_spmd, body=%wide.region_10.0_spmd.sunk | while | flops 3221749760 | bytes 7341298 | solution.py:28
  219.6 0.6 dynamic_slice.56
  221.9 0.7 and_reduce_fusion.5
  222.6 3.4 %fusion.50 = f32[512,512]{1,0:T(8,128)S(1)} fusion(f32[512,512]{1,0:T(8,128)} %get-tuple-element.299, f32[4,512,512]{2,1,0:T(8,128)} %get-tuple-element.298, s32[]{:T(128)S(6)} %select_n.30), kind=kOutput, calls=%fused_computation.15.clone.1 | convolution fusion | flops 1610612736 | bytes 3145732 | tf_op jit(solution)/shard_map/while/body/dot_general | solution.py:14
  226.0 3.7 %fusion.51 = f32[512,3,512]{2,0,1:T(8,128)S(1)} fusion(f32[512,3,512]{2,0,1:T(8,128)S(1)} %get-tuple-element.282, s32[]{:T(128)} %select_n.31, f32[512,512]{1,0:T(8,128)S(1)} %fusion.50, f32[4,512,512]{2,1,0:T(8,128)} %get-tuple-element.300, s32[]{:T(128)S(6)} %select_n.30, pred[]{:T(512)} %and_reduce_fusion.5), kind=kOutput, calls=%fused_computation.13.clone.1 | convolution fusion | flops 1611137024 | bytes 4195332 | tf_op jit(solution)/shard_map/while/body/dot_general | solution.py:14
  230.3 0.2 slice_bitcast_fusion.1
  230.5 1.6 collective-permute-start.2
  232.2 1.3 collective-permute-start.3
  233.5 0.9 collective-permute-done.2
  234.4 3.7 %collective-permute-done.3 = f32[512,512]{1,0:T(8,128)S(1)} collective-permute-done((f32[512,512]{1,0:T(8,128)S(1)}, f32[512,512]{1,0:T(8,128)S(1)}, u32[]{:S(2)}, u32[]{:S(2)}) %collective-permute-start.3) | collective-permute-done | bytes 1048608 | tf_op jit(solution)/shard_map/ppermute | solution.py:10
  238.1 1.4 fusion.16
  239.5 0.0 reduce-scatter.5.cloned.1.call-update
  239.5 70.2 %reduce-scatter.5.cloned.1.call-done = f32[128,512]{1,0:T(8,128)} async-done(((f32[512,512]{1,0:T(8,128)}), f32[128,512]{1,0:T(8,128)}) %reduce-scatter.5.cloned.1.call-update) | async-done | bytes 262160 | tf_op jit(solution)/shard_map/reduce_scatter | solution.py:50
Async XLA Ops:
  7.2 1.1 copy-start.1
  7.2 96.0 %reduce-scatter.3.cloned.1.call-start = ((), (), s32[]{:S(2)}) async-start(), calls=%async_computation.2 | async-start | bytes 1310720 | tf_op jit(solution)/shard_map/reduce_scatter | solution.py:50
  20.2 125.5 %copy-start = (f32[1,128,512]{2,1,0:T(8,128)S(1)}, f32[1,128,512]{2,1,0:T(8,128)}, u32[]{:S(2)}) copy-start(f32[1,128,512]{2,1,0:T(8,128)} %param.15) | copy-start | bytes 786436
  20.2 4.8 %collective-permute-start = (f32[512,512]{1,0:T(8,128)S(1)}, f32[512,512]{1,0:T(8,128)S(1)}, u32[]{:S(2)}, u32[]{:S(2)}) collective-permute-start(f32[512,512]{1,0:T(8,128)S(1)} %get-tuple-element.139), channel_id=1, source_target_pairs={{0,1},{1,2},{2,3},{3,4},{4,5},{5,6},{6,7},{8,9},{9,10},{10,11},{11... | collective-permute-start | bytes 3145736 | tf_op jit(solution)/shard_map/ppermute | solution.py:10
  22.8 6.7 %collective-permute-start.1 = (f32[512,512]{1,0:T(8,128)S(1)}, f32[512,512]{1,0:T(8,128)S(1)}, u32[]{:S(2)}, u32[]{:S(2)}) collective-permute-start(f32[512,512]{1,0:T(8,128)S(1)} %get-tuple-element.140), channel_id=1, source_target_pairs={{1,0},{2,1},{3,2},{4,3},{5,4},{6,5},{7,6},{9,8},{10,9},{11,10},{12... | collective-permute-start | bytes 3145736 | tf_op jit(solution)/shard_map/ppermute | solution.py:10
  30.9 187.7 %all-gather.2.cloned.1.call-start = ((), (), s32[]{:S(2)}) async-start(), calls=%async_computation.3 | async-start | bytes 1310720 | tf_op jit(solution)/shard_map/all_gather | solution.py:64
  192.0 117.7 %reduce-scatter.5.cloned.1.call-start = ((), (), s32[]{:S(2)}) async-start(), calls=%async_computation.4 | async-start | bytes 1310720 | tf_op jit(solution)/shard_map/reduce_scatter | solution.py:50
  230.5 3.8 %collective-permute-start.2 = (f32[512,512]{1,0:T(8,128)S(1)}, f32[512,512]{1,0:T(8,128)S(1)}, u32[]{:S(2)}, u32[]{:S(2)}) collective-permute-start(f32[512,512]{1,0:T(8,128)S(1)} %get-tuple-element.137), channel_id=1, source_target_pairs={{0,1},{1,2},{2,3},{3,4},{4,5},{5,6},{6,7},{8,9},{9,10},{10,11},{11... | collective-permute-start | bytes 3145736 | tf_op jit(solution)/shard_map/ppermute | solution.py:10
  232.2 5.9 %collective-permute-start.3 = (f32[512,512]{1,0:T(8,128)S(1)}, f32[512,512]{1,0:T(8,128)S(1)}, u32[]{:S(2)}, u32[]{:S(2)}) collective-permute-start(f32[512,512]{1,0:T(8,128)S(1)} %get-tuple-element.138), channel_id=1, source_target_pairs={{1,0},{2,1},{3,2},{4,3},{5,4},{6,5},{7,6},{9,8},{10,9},{11,10},{12... | collective-permute-start | bytes 3145736 | tf_op jit(solution)/shard_map/ppermute | solution.py:10
Sparse Core Ops, SparseCore 0:
  31.0 72.1 reduce-scatter.2
  192.1 26.4 all-gather.1
  239.6 69.9 reduce-scatter.4
where the time goes:
time: 318 us; the launch traced here: 316 us
  waiting for transfers between devices  179 us (56%)
  blocking collectives  80.9 us (25%)
  between operations  16.5 us (5%)
  matrix products  14.2 us (4%)
  other arithmetic  10 us (3%)
  starting transfers between devices  6.94 us (2%)
  loops' own time  6.29 us (2%)
    reduce_scatter x2, waiting for transfers between devices, apply_hamiltonian(): lax.psum_scatter(whole[:, 1] + upward + downward, 'term', scatter_dimensi...  142 us
    psum x1, blocking collectives, per_device(): correlation_sum = lax.psum(jnp.sum(own_rows * raw), ('term', 'sector'))  41.3 us
    psum x1, blocking collectives, per_device(): lax.psum((jnp.sum(own_rows * first_image), jnp.sum(own_rows * own_rows)),...  39.5 us
    all_gather x1, waiting for transfers between devices, per_device(): full_correction = lax.all_gather(correction, 'term', axis=0, tiled=True)  26.5 us
    dot_general x4, matrix products, matmul(): jnp.dot(first_op, second_op, precision=lax.Precision.HIGHEST, preferred_e...  14.2 us
    ppermute x4, waiting for transfers between devices, from_behind(): return lax.ppermute(block, axis, route)  10 us
    ppermute x4, starting transfers between devices, from_behind(): return lax.ppermute(block, axis, route)  6.82 us
  transfers between devices with their start and end apart: 7, of which 7 were waited for; matrix products, arithmetic and copies ran while one was open for 0% of the time, Pallas kernels for 0%

commit v1 on v0

--- a/solution.py
+++ b/solution.py
@@ -30,6 +30,12 @@
 
 
 def per_device(wavefunction, precond, left_ops, right_ops, out_sector, live_counts):
+
+    def track_rates(u_in):
+        for src_i in ("sector", "term"):
+            u_in = jax.lax.psum(u_in, src_i)
+        return u_in
+
     term_count = lax.axis_size("term")
     width = wavefunction.shape[1]
     slab_rows = width // term_count
@@ -54,9 +60,7 @@
     first_image = apply_hamiltonian(center)
     own_rows = lax.dynamic_slice_in_dim(center, first_own, slab_rows, 0)
     scaling = precond[0]
-    cross, norm_sq = lax.psum(
-        (jnp.sum(own_rows * first_image), jnp.sum(own_rows * own_rows)), ("term", "sector")
-    )
+    cross, norm_sq = track_rates((jnp.sum(own_rows * first_image), jnp.sum(own_rows * own_rows)))
     rayleigh = cross / norm_sq
     raw = scaling * (first_image - rayleigh * own_rows)
     correlation_sum = lax.psum(jnp.sum(own_rows * raw), ("term", "sector"))

time: 318 us -> 302 us (0.950)
  blocking collectives: 80.9 us -> 63.3 us
    psum x1 -> x2, blocking collectives: 39.5 us -> 26.3 us  [track_rates(): u_in = jax.lax.psum(u_in, src_i)]
    psum x1, blocking collectives: 41.3 us -> 37 us  [per_device(): correlation_sum = lax.psum(jnp.sum(own_rows * raw), ('term', 'sector'))]
where the time goes in v1:
time: 302 us; the launch traced here: 300 us
  waiting for transfers between devices  181 us (60%)
  blocking collectives  63.3 us (21%)
  between operations  16.5 us (5%)
  matrix products  14.2 us (5%)
  other arithmetic  10 us (3%)
  starting transfers between devices  6.94 us (2%)
  loops' own time  6.29 us (2%)
    reduce_scatter x2, waiting for transfers between devices, apply_hamiltonian(): lax.psum_scatter(whole[:, 1] + upward + downward, 'term', scatter_dimensi...  142 us
    psum x1, blocking collectives, per_device(): correlation_sum = lax.psum(jnp.sum(own_rows * raw), ('term', 'sector'))  37 us
    all_gather x1, waiting for transfers between devices, per_device(): full_correction = lax.all_gather(correction, 'term', axis=0, tiled=True)  28.1 us
    psum x2, blocking collectives, track_rates(): u_in = jax.lax.psum(u_in, src_i)  26.3 us
    dot_general x4, matrix products, matmul(): jnp.dot(first_op, second_op, precision=lax.Precision.HIGHEST, preferred_e...  14.2 us
    ppermute x4, waiting for transfers between devices, from_behind(): return lax.ppermute(block, axis, route)  9.99 us
    ppermute x4, starting transfers between devices, from_behind(): return lax.ppermute(block, axis, route)  6.82 us
    another operation x2, loops' own time, term_rows(): totals = lax.fori_loop(jnp.zeros((), jnp.int32), kept, add_slot, totals)  6.29 us
  transfers between devices with their start and end apart: 7, of which 7 were waited for; matrix products, arithmetic and copies ran while one was open for 0% of the time, Pallas kernels for 0%

profile of v1, /device:TPU:0, one launch (start us, length us, event | category | flops | bytes accessed | tf_op | source)
XLA Modules:
  0.0 300.2 jit_solution(5773341315803560178)
XLA Ops:
  7.2 0.0 copy-start.1
  7.2 0.0 reduce-scatter.3.cloned.1.call-start
  7.2 0.7 add_bitcast_fusion
  7.9 0.4 broadcast.48.clone
  8.3 0.0 copy-done.1
  8.3 11.7 %while.22 = (s32[]{:T(128)}, f32[512,3,512]{2,0,1:T(8,128)S(1)}, s32[]{:T(128)}, s32[4]{0:T(128)S(1)}, f32[4,512,512]{2,1,0:T(8,128)}, /*index=5*/f32[512,512]{1...) while((s32[]{:T(128)}, f32[512,3,512]{2,0,1:T(8,128)S(1)}, ...), condition=%wide.region_2.0_spmd, body=%wide.region_0.0_spmd.sunk | while | flops 3221749760 | bytes 7341298 | solution.py:28
  9.0 0.6 dynamic_slice.53
  11.5 0.7 and_reduce_fusion.4
  12.2 3.4 %fusion.44 = f32[512,512]{1,0:T(8,128)S(1)} fusion(f32[512,512]{1,0:T(8,128)} %get-tuple-element.262, f32[4,512,512]{2,1,0:T(8,128)} %get-tuple-element.261, s32[]{:T(128)S(6)} %select_n.28), kind=kOutput, calls=%fused_computation.4.clone.1 | convolution fusion | flops 1610612736 | bytes 3145732 | tf_op jit(solution)/shard_map/while/body/dot_general | solution.py:14
  15.6 3.8 %fusion.45 = f32[512,3,512]{2,0,1:T(8,128)S(1)} fusion(f32[512,3,512]{2,0,1:T(8,128)S(1)} %get-tuple-element.245, s32[]{:T(128)} %select_n.29, f32[512,512]{1,0:T(8,128)S(1)} %fusion.44, f32[4,512,512]{2,1,0:T(8,128)} %get-tuple-element.263, s32[]{:T(128)S(6)} %select_n.28, pred[]{:T(512)} %and_reduce_fusion.4), kind=kOutput, calls=%fused_computation.2.clone.1 | convolution fusion | flops 1611137024 | bytes 4195332 | tf_op jit(solution)/shard_map/while/body/dot_general | solution.py:14
  20.0 0.2 slice_bitcast_fusion.3
  20.2 0.0 copy-start
  20.2 2.6 collective-permute-start
  22.8 1.3 collective-permute-start.1
  24.1 0.9 collective-permute-done
  25.0 4.5 %collective-permute-done.1 = f32[512,512]{1,0:T(8,128)S(1)} collective-permute-done((f32[512,512]{1,0:T(8,128)S(1)}, f32[512,512]{1,0:T(8,128)S(1)}, u32[]{:S(2)}, u32[]{:S(2)}) %collective-permute-start.1) | collective-permute-done | bytes 1048608 | tf_op jit(solution)/shard_map/ppermute | solution.py:10
  29.5 1.4 fusion.17
  30.9 0.0 reduce-scatter.3.cloned.1.call-update
  30.9 0.0 all-gather.2.cloned.1.call-start
  30.9 72.2 %reduce-scatter.3.cloned.1.call-done = f32[128,512]{1,0:T(8,128)} async-done(((f32[512,512]{1,0:T(8,128)}), f32[128,512]{1,0:T(8,128)}) %reduce-scatter.3.cloned.1.call-update) | async-done | bytes 262160 | tf_op jit(solution)/shard_map/reduce_scatter | solution.py:56
  103.2 1.7 fusion.19
  104.9 16.8 %all-reduce = (f32[]{:T(128)}, f32[]{:T(128)}) all-reduce(f32[]{:T(128)} %get-tuple-element.106, f32[]{:T(128)} %get-tuple-element.105), channel_id=1, replica_groups=mesh['term'=4,'sector'=8] {'sector'}, use_global_device_ids=true, to_apply=%region_5.0 | all-reduce | flops 2 | bytes 16 | tf_op jit(solution)/shard_map/psum | solution.py:36
  121.7 9.6 %all-reduce.1 = (f32[]{:T(128)}, f32[]{:T(128)}) all-reduce(f32[]{:T(128)} %get-tuple-element.135, f32[]{:T(128)} %get-tuple-element.136), channel_id=1, replica_groups=mesh['term'=4,'sector'=8] {'term'}, use_global_device_ids=true, to_apply=%region_6.0 | all-reduce | flops 2 | bytes 16 | tf_op jit(solution)/shard_map/psum | solution.py:36
  132.6 0.0 copy-done
  132.6 1.7 fusion.22
  134.3 37.0 %psum.39 = f32[]{:T(128)} all-reduce(f32[]{:T(128)} %fusion.22), channel_id=1, replica_groups=mesh['term'=4,'sector'=8] {'term','sector'}, use_global_device_ids=true, to_apply=%region_11.0 | all-reduce | flops 1 | bytes 8 | tf_op jit(solution)/shard_map/psum | solution.py:66
  172.6 1.8 fusion.23
  174.4 0.0 all-gather.2.cloned.1.call-update
  174.5 0.0 reduce-scatter.5.cloned.1.call-start
  174.5 28.1 %all-gather.2.cloned.1.call-done = f32[512,512]{1,0:T(8,128)} async-done(((f32[128,512]{1,0:T(8,128)}), f32[512,512]{1,0:T(8,128)}) %all-gather.2.cloned.1.call-update) | async-done | bytes 1048592 | tf_op jit(solution)/shard_map/all_gather | solution.py:68
  202.6 0.4 broadcast.48
  203.0 11.4 %while.23 = (s32[]{:T(128)}, f32[512,3,512]{2,0,1:T(8,128)S(1)}, s32[]{:T(128)}, s32[4]{0:T(128)S(1)}, f32[4,512,512]{2,1,0:T(8,128)}, /*index=5*/f32[512,512]{1...) while((s32[]{:T(128)}, f32[512,3,512]{2,0,1:T(8,128)S(1)}, ...), condition=%wide.region_14.0_spmd, body=%wide.region_12.0_spmd.sunk | while | flops 3221749760 | bytes 7341298 | solution.py:28
  203.7 0.6 dynamic_slice.56
  206.0 0.7 and_reduce_fusion.5
  206.7 3.4 %fusion.50 = f32[512,512]{1,0:T(8,128)S(1)} fusion(f32[512,512]{1,0:T(8,128)} %get-tuple-element.301, f32[4,512,512]{2,1,0:T(8,128)} %get-tuple-element.300, s32[]{:T(128)S(6)} %select_n.30), kind=kOutput, calls=%fused_computation.15.clone.1 | convolution fusion | flops 1610612736 | bytes 3145732 | tf_op jit(solution)/shard_map/while/body/dot_general | solution.py:14
  210.1 3.7 %fusion.51 = f32[512,3,512]{2,0,1:T(8,128)S(1)} fusion(f32[512,3,512]{2,0,1:T(8,128)S(1)} %get-tuple-element.284, s32[]{:T(128)} %select_n.31, f32[512,512]{1,0:T(8,128)S(1)} %fusion.50, f32[4,512,512]{2,1,0:T(8,128)} %get-tuple-element.302, s32[]{:T(128)S(6)} %select_n.30, pred[]{:T(512)} %and_reduce_fusion.5), kind=kOutput, calls=%fused_computation.13.clone.1 | convolution fusion | flops 1611137024 | bytes 4195332 | tf_op jit(solution)/shard_map/while/body/dot_general | solution.py:14
  214.4 0.2 slice_bitcast_fusion.1
  214.6 1.6 collective-permute-start.2
  216.2 1.3 collective-permute-start.3
  217.5 0.9 collective-permute-done.2
  218.5 3.7 %collective-permute-done.3 = f32[512,512]{1,0:T(8,128)S(1)} collective-permute-done((f32[512,512]{1,0:T(8,128)S(1)}, f32[512,512]{1,0:T(8,128)S(1)}, u32[]{:S(2)}, u32[]{:S(2)}) %collective-permute-start.3) | collective-permute-done | bytes 1048608 | tf_op jit(solution)/shard_map/ppermute | solution.py:10
  222.2 1.4 fusion.16
  223.5 0.0 reduce-scatter.5.cloned.1.call-update
  223.6 70.2 %reduce-scatter.5.cloned.1.call-done = f32[128,512]{1,0:T(8,128)} async-done(((f32[512,512]{1,0:T(8,128)}), f32[128,512]{1,0:T(8,128)}) %reduce-scatter.5.cloned.1.call-update) | async-done | bytes 262160 | tf_op jit(solution)/shard_map/reduce_scatter | solution.py:56
Async XLA Ops:
  7.2 1.1 copy-start.1
  7.2 96.0 %reduce-scatter.3.cloned.1.call-start = ((), (), s32[]{:S(2)}) async-start(), calls=%async_computation.2 | async-start | bytes 1310720 | tf_op jit(solution)/shard_map/reduce_scatter | solution.py:56
  20.2 112.3 %copy-start = (f32[1,128,512]{2,1,0:T(8,128)S(1)}, f32[1,128,512]{2,1,0:T(8,128)}, u32[]{:S(2)}) copy-start(f32[1,128,512]{2,1,0:T(8,128)} %param.15) | copy-start | bytes 786436
  20.2 4.8 %collective-permute-start = (f32[512,512]{1,0:T(8,128)S(1)}, f32[512,512]{1,0:T(8,128)S(1)}, u32[]{:S(2)}, u32[]{:S(2)}) collective-permute-start(f32[512,512]{1,0:T(8,128)S(1)} %get-tuple-element.141), channel_id=1, source_target_pairs={{0,1},{1,2},{2,3},{3,4},{4,5},{5,6},{6,7},{8,9},{9,10},{10,11},{11... | collective-permute-start | bytes 3145736 | tf_op jit(solution)/shard_map/ppermute | solution.py:10
  22.8 6.7 %collective-permute-start.1 = (f32[512,512]{1,0:T(8,128)S(1)}, f32[512,512]{1,0:T(8,128)S(1)}, u32[]{:S(2)}, u32[]{:S(2)}) collective-permute-start(f32[512,512]{1,0:T(8,128)S(1)} %get-tuple-element.142), channel_id=1, source_target_pairs={{1,0},{2,1},{3,2},{4,3},{5,4},{6,5},{7,6},{9,8},{10,9},{11,10},{12... | collective-permute-start | bytes 3145736 | tf_op jit(solution)/shard_map/ppermute | solution.py:10
  30.9 171.7 %all-gather.2.cloned.1.call-start = ((), (), s32[]{:S(2)}) async-start(), calls=%async_computation.3 | async-start | bytes 1310720 | tf_op jit(solution)/shard_map/all_gather | solution.py:68
  174.5 119.3 %reduce-scatter.5.cloned.1.call-start = ((), (), s32[]{:S(2)}) async-start(), calls=%async_computation.4 | async-start | bytes 1310720 | tf_op jit(solution)/shard_map/reduce_scatter | solution.py:56
  214.6 3.9 %collective-permute-start.2 = (f32[512,512]{1,0:T(8,128)S(1)}, f32[512,512]{1,0:T(8,128)S(1)}, u32[]{:S(2)}, u32[]{:S(2)}) collective-permute-start(f32[512,512]{1,0:T(8,128)S(1)} %get-tuple-element.139), channel_id=1, source_target_pairs={{0,1},{1,2},{2,3},{3,4},{4,5},{5,6},{6,7},{8,9},{9,10},{10,11},{11... | collective-permute-start | bytes 3145736 | tf_op jit(solution)/shard_map/ppermute | solution.py:10
  216.2 5.9 %collective-permute-start.3 = (f32[512,512]{1,0:T(8,128)S(1)}, f32[512,512]{1,0:T(8,128)S(1)}, u32[]{:S(2)}, u32[]{:S(2)}) collective-permute-start(f32[512,512]{1,0:T(8,128)S(1)} %get-tuple-element.140), channel_id=1, source_target_pairs={{1,0},{2,1},{3,2},{4,3},{5,4},{6,5},{7,6},{9,8},{10,9},{11,10},{12... | collective-permute-start | bytes 3145736 | tf_op jit(solution)/shard_map/ppermute | solution.py:10
Sparse Core Ops, SparseCore 0:
  31.0 72.1 reduce-scatter.2
  174.6 28.0 all-gather.1
  223.7 69.9 reduce-scatter.4
